TPU v7x, 128 devices: a whole 4x4x4 slice. The times are simulated.
128 devices in a mesh: grp: 2 (over x_lo), dp: 64 (over y, x_hi, z, core).
Axes of the slice: x: 4 (x_hi: 2, x_lo: 2; x = x_hi * 2 + x_lo), y: 4, z: 4, core: 2. Of those that a mesh axis runs over, the one named last changes fastest.
Arguments:
- teacher_in: bfloat16 [32768, 1664], P('dp'), may hold values from -6 to 6
- teacher_gain: float32 [1664], replicated, may hold values from 0.5 to 1.5
- teacher_up: bfloat16 [1664, 4096], P('dp', 'grp'), may hold values from -0.15625 to 0.15625
- teacher_down: bfloat16 [1664, 4096], P('dp', 'grp'), may hold values from -0.09375 to 0.09375
- student_in: bfloat16 [32768, 768], P('dp'), may hold values from -6 to 6
- student_gain: float32 [768], replicated, may hold values from 0.5 to 1.5
- student_up: bfloat16 [768, 1536], P(None, ('grp', 'dp')), may hold values from -0.21875 to 0.21875
- student_down: bfloat16 [1536, 768], P(('grp', 'dp')), may hold values from -0.15625 to 0.15625
- student_head: bfloat16 [768, 1664], P(None, ('grp', 'dp')), may hold values from -0.21875 to 0.21875
- student_proj: bfloat16 [768, 512], P(None, ('grp', 'dp')), may hold values from -1 to 1
- word_table: bfloat16 [49408, 512], P(('grp', 'dp')), may hold values from -6 to 6
- caption_ids: int32 [128, 77], replicated, may hold values from 0 to 49407
- positive: int32 [128], replicated, may hold values from 0 to 127, each once
Outputs:
- loss: float32 [], replicated
- grad_up: float32 [768, 1536], P(None, ('grp', 'dp'))
- grad_down: float32 [1536, 768], P(('grp', 'dp'))
- grad_head: float32 [768, 1664], P(None, ('grp', 'dp'))
- grad_proj: float32 [768, 512], P(None, ('grp', 'dp'))
Inputs may be any that keep to these rules, and one draw needn't show every extreme that they name: Each caption is the positive of exactly one image.
All inputs are finite; a program needn't handle non-finite values.
Results may differ from a plain program's by a relative error of at most 0.0065.
Values may be sent and summed in bfloat16 or wider, within the bound.
A program may use at most 128 MiB of HBM per device.

v0:
```python
import jax
import jax.numpy as jnp
from jax import lax
from jax.sharding import PartitionSpec as P

CAP_LEN = 77
PATCHES = 256
IMG_DEV = 1


def normalize_rows(values, gain):
    center = values - jnp.mean(values, -1, keepdims=True)
    spread = jnp.mean(center * center, -1, keepdims=True)
    return center * lax.rsqrt(spread + 1e-05) * gain


def gelu_tanh(values):
    return jax.nn.gelu(values, approximate=True)


def unit_rows(values):
    return values / jnp.sqrt(jnp.sum(values * values, -1, keepdims=True) + 1e-06)


def local(
    teacher_in,
    teacher_gain,
    teacher_up,
    teacher_down,
    student_in,
    student_gain,
    student_up,
    student_down,
    student_head,
    student_proj,
    word_table,
    caption_ids,
    positive,
):
    contract = (((1,), (1,)), ((), ()))
    grp_index = lax.axis_index("grp")
    dp_index = lax.axis_index("dp")
    n_grp = lax.axis_size("grp")
    n_dp = lax.axis_size("dp")
    devices = n_grp * n_dp
    teacher_width = teacher_in.shape[1]
    rows_teacher = teacher_in.shape[0]
    teacher_normed = normalize_rows(teacher_in.astype(jnp.float32), teacher_gain).astype(
        jnp.bfloat16
    )
    columns = teacher_normed
    hidden = jnp.dot(
        columns,
        lax.all_gather(teacher_up, "dp", axis=0, tiled=True),
        preferred_element_type=jnp.float32,
    )
    teacher_act = gelu_tanh(hidden).astype(jnp.bfloat16)
    partial_value = lax.dot_general(
        teacher_act,
        lax.all_gather(teacher_down, "dp", axis=0, tiled=True),
        contract,
        preferred_element_type=jnp.float32,
    )
    branch = lax.psum_scatter(
        partial_value.astype(jnp.bfloat16), "grp", scatter_dimension=0, tiled=True
    ).astype(jnp.float32)
    own_rows = rows_teacher // n_grp
    target = (
        lax.dynamic_slice_in_dim(teacher_in, grp_index * own_rows, own_rows, 0).astype(jnp.float32)
        + branch
    )
    student_rows = lax.dynamic_slice_in_dim(student_in, grp_index * own_rows, own_rows, 0).astype(
        jnp.float32
    )
    student_width = student_rows.shape[1]
    student_normed = normalize_rows(student_rows, student_gain).astype(jnp.bfloat16)
    gate_out = jnp.dot(
        student_normed,
        lax.all_gather(student_up, ("grp", "dp"), axis=1, tiled=True),
        preferred_element_type=jnp.float32,
    )
    down_whole, head_whole, proj_whole = (
        lax.all_gather(student_down, ("grp", "dp"), axis=0, tiled=True),
        lax.all_gather(student_head, ("grp", "dp"), axis=1, tiled=True),
        lax.all_gather(student_proj, ("grp", "dp"), axis=1, tiled=True),
    )
    student_act = gelu_tanh(gate_out).astype(jnp.bfloat16)
    student_out = student_rows + jnp.dot(
        student_act, down_whole, preferred_element_type=jnp.float32
    )
    student_rounded = student_out.astype(jnp.bfloat16)
    diff = jnp.dot(student_rounded, head_whole, preferred_element_type=jnp.float32) - target
    feature_part = jnp.sum(diff * diff) / teacher_width
    pooled = (jnp.sum(student_out.reshape(IMG_DEV, PATCHES, student_width), 1) / PATCHES).astype(
        jnp.bfloat16
    )
    projected = jnp.dot(pooled, proj_whole, preferred_element_type=jnp.float32)
    proj_norm = jnp.sqrt(jnp.sum(projected * projected, -1, keepdims=True) + 1e-06)
    image_emb = projected / proj_norm
    embed_width = image_emb.shape[1]
    caption_count = caption_ids.shape[0]
    caption_dev = caption_count // devices
    shard_block = grp_index * n_dp + dp_index
    vocab_dev = word_table.shape[0]
    vocab_codes = shard_block * vocab_dev + jnp.arange(vocab_dev, dtype=jnp.int32)
    counts = jnp.sum(
        caption_ids[:, :, None] == vocab_codes[None, None, :], 1, dtype=jnp.float32
    ).astype(jnp.bfloat16)
    partial_words = jnp.dot(counts, word_table, preferred_element_type=jnp.float32) / CAP_LEN
    words = lax.psum(partial_words, ("grp", "dp"))
    caption_all = unit_rows(words)
    caption_own = lax.dynamic_slice_in_dim(caption_all, shard_block * caption_dev, caption_dev, 0)
    gathered = lax.all_gather(image_emb, ("grp", "dp"), axis=0, tiled=True)
    image_all = jnp.transpose(
        gathered.reshape(n_grp, n_dp, IMG_DEV, embed_width), (1, 0, 2, 3)
    ).reshape(-1, embed_width)
    image_first = (dp_index * n_grp + grp_index) * IMG_DEV
    positive_own = lax.dynamic_slice_in_dim(positive, image_first, IMG_DEV, 0)
    scores_own = 100.0 * jnp.dot(image_emb, caption_all.T, precision=lax.Precision.HIGHEST)
    match_own = (
        positive_own[:, None] == jnp.arange(caption_count, dtype=jnp.int32)[None, :]
    ).astype(jnp.float32)
    caption_first = shard_block * caption_dev
    scores_cols = 100.0 * jnp.dot(image_all, caption_own.T, precision=lax.Precision.HIGHEST)
    match_cols = (
        positive[:, None] == (caption_first + jnp.arange(caption_dev, dtype=jnp.int32))[None, :]
    ).astype(jnp.float32)
    contrast_part = jnp.sum(jax.nn.logsumexp(scores_own, 1)) - jnp.sum(match_own * scores_own)
    contrast_part = (
        contrast_part
        + jnp.sum(jax.nn.logsumexp(scores_cols, 0))
        - jnp.sum(match_cols * scores_cols)
    )
    grad_rows = jax.nn.softmax(scores_own, 1) - match_own
    grad_cols = jax.nn.softmax(scores_cols, 0) - match_cols
    grad_far = 100.0 * jnp.dot(grad_cols, caption_own, precision=lax.Precision.HIGHEST)
    grad_far = jnp.transpose(
        grad_far.reshape(n_dp, n_grp, IMG_DEV, embed_width), (1, 0, 2, 3)
    ).reshape(-1, embed_width)
    grad_image = 100.0 * jnp.dot(grad_rows, caption_all, precision=lax.Precision.HIGHEST)
    grad_image = grad_image + lax.psum_scatter(
        grad_far, ("grp", "dp"), scatter_dimension=0, tiled=True
    )
    grad_projected = (
        (grad_image - image_emb * jnp.sum(image_emb * grad_image, -1, keepdims=True)) / proj_norm
    ).astype(jnp.bfloat16)
    proj_part = jnp.dot(pooled.T, grad_projected, preferred_element_type=jnp.float32)
    grad_pooled = lax.dot_general(
        grad_projected, proj_whole, contract, preferred_element_type=jnp.float32
    )
    grad_pred = (2.0 * diff / teacher_width).astype(jnp.bfloat16)
    head_part = jnp.dot(student_rounded.T, grad_pred, preferred_element_type=jnp.float32)
    grad_out = lax.dot_general(grad_pred, head_whole, contract, preferred_element_type=jnp.float32)
    grad_out = (
        (grad_out.reshape(IMG_DEV, PATCHES, student_width) + (grad_pooled / PATCHES)[:, None, :])
        .reshape(-1, student_width)
        .astype(jnp.bfloat16)
    )
    columns = student_act
    grad_down = lax.psum_scatter(
        lax.dot_general(
            columns, grad_out, (((0,), (0,)), ((), ())), preferred_element_type=jnp.float32
        ),
        ("grp", "dp"),
        scatter_dimension=0,
        tiled=True,
    )
    grad_act = lax.dot_general(grad_out, down_whole, contract, preferred_element_type=jnp.float32)
    grad_gate = jax.vjp(gelu_tanh, gate_out)[1](grad_act)[0].astype(jnp.bfloat16)
    up_part = jnp.dot(student_normed.T, grad_gate, preferred_element_type=jnp.float32)
    grad_up, grad_head, grad_proj = (
        lax.psum_scatter(up_part, ("grp", "dp"), scatter_dimension=1, tiled=True),
        lax.psum_scatter(head_part, ("grp", "dp"), scatter_dimension=1, tiled=True),
        lax.psum_scatter(proj_part, ("grp", "dp"), scatter_dimension=1, tiled=True),
    )
    total = lax.psum(feature_part + contrast_part, ("grp", "dp"))
    loss = total / (positive.shape[0] * PATCHES)
    return (loss, grad_up, grad_down, grad_head, grad_proj)


def solution(mesh):
    placed = (
        P("dp", None),
        P(),
        P("dp", "grp"),
        P("dp", "grp"),
        P("dp", None),
        P(),
        P(None, ("grp", "dp")),
        P(("grp", "dp"), None),
        P(None, ("grp", "dp")),
        P(None, ("grp", "dp")),
        P(("grp", "dp"), None),
        P(),
        P(),
    )
    return jax.shard_map(
        local,
        mesh=mesh,
        in_specs=placed,
        out_specs=(
            P(),
            P(None, ("grp", "dp")),
            P(("grp", "dp"), None),
            P(None, ("grp", "dp")),
            P(None, ("grp", "dp")),
        ),
        check_vma=False,
    )
```

profile of v0, /device:TPU:16, one launch (start us, length us, event | category | flops | bytes accessed | tf_op | source)
XLA Modules:
  0.0 1861.4 jit_solution(75165170728293733)
XLA Ops:
  13.5 164.2 %all-gather.6 = bf16[128,4,768]{2,1,0:T(4,128)(2,1)S(1)} all-gather(bf16[1,4,768]{2,1,0:T(4,128)(2,1)} %bitcast.97), channel_id=1, replica_groups=mesh['grp'=2,'dp'=64] {'grp','dp'}, dimensions={0}, use_global_device_ids=true | all-gather | bytes 792576 | tf_op jit(solution)/shard_map/all_gather | solution.py:85
  181.1 172.8 %all-gather.16.cloned.1.call-done = bf16[128,12,768]{2,1,0:T(8,128)(2,1)} async-done(((bf16[1,12,768]{2,1,0:T(8,128)(2,1)}), bf16[128,12,768]{2,1,0:T(8,128)(2,1)}) %all-gather.16.cloned.1.call-update) | async-done | bytes 2359312 | tf_op jit(solution)/shard_map/all_gather | solution.py:83
  353.8 4.9 reshape.194
  358.8 192.1 %all-gather.14.cloned.1.call-done = bf16[128,12,768]{2,1,0:T(8,128)(2,1)} async-done(((bf16[1,12,768]{2,1,0:T(8,128)(2,1)}), bf16[128,12,768]{2,1,0:T(8,128)(2,1)}) %all-gather.14.cloned.1.call-update) | async-done | bytes 2359312 | tf_op jit(solution)/shard_map/all_gather | solution.py:79
  550.9 4.9 reshape.192
  562.9 161.3 %all-gather.7 = f32[128,1,512]{2,1,0:T(1,128)S(1)} all-gather(f32[1,1,512]{2,1,0:T(1,128)S(1)} %bitcast.84), channel_id=2, replica_groups=mesh['grp'=2,'dp'=64] {'grp','dp'}, dimensions={0}, use_global_device_ids=true | all-gather | bytes 264192 | tf_op jit(solution)/shard_map/all_gather | solution.py:113
  740.5 9.1 reshape.200
  749.6 9.1 reshape.198
  758.7 14.6 convolution_convert_fusion
  775.8 114.0 %all-reduce.15.cloned.1.call-done = f32[128,512]{1,0:T(8,128)} async-done(((f32[128,512]{1,0:T(8,128)}), f32[128,512]{1,0:T(8,128)}) %all-reduce.15.cloned.1.call-update) | async-done | bytes 262160
  894.2 191.6 %all-gather.18.cloned.1.call-done = bf16[128,13,768]{2,1,0:T(8,128)(2,1)} async-done(((bf16[1,13,768]{2,1,0:T(8,128)(2,1)}), bf16[128,13,768]{2,1,0:T(8,128)(2,1)}) %all-gather.18.cloned.1.call-update) | async-done | bytes 2555920 | tf_op jit(solution)/shard_map/all_gather | solution.py:84
  1085.8 5.3 reshape.196
  1091.2 26.4 %reduce-scatter.8.cloned.1.call-done = bf16[256,1664]{1,0:T(8,128)(2,1)} async-done(((bf16[512,1664]{1,0:T(8,128)(2,1)}), bf16[256,1664]{1,0:T(8,128)(2,1)}) %reduce-scatter.8.cloned.1.call-update) | async-done | bytes 851984 | tf_op jit(solution)/shard_map/reduce_scatter | solution.py:64
  1117.5 3.9 multiply_reduce_fusion
  1123.8 6.2 fusion.45
  1136.5 335.6 %fusion.88 = (f32[768,16]{0,1:T(8,128)S(1)}, f32[16,768]{1,0:T(8,128)S(1)}, f32[768,16]{0,1:T(8,128)S(1)}) fusion(f32[768,1536]{0,1:T(8,128)} %fusion.45, f32[1536,768]{1,0:T(8,128)} %fusion.87, f32[768,1664]{0,1:T(8,128)} %fusion.56), kind=kCustom, calls=%all-reduce-scatter.3 | all-reduce-scatter fusion | flops 4718593 | bytes 14696448
  1476.0 9.8 collective-permute-start.63
  1485.8 26.3 %collective-permute-start.30 = (f32[768,16]{0,1:T(8,128)S(1)}, f32[768,16]{0,1:T(8,128)S(1)}, u32[]{:S(2)}, u32[]{:S(2)}) collective-permute-start(f32[768,16]{0,1:T(8,128)S(1)} %get-tuple-element.14), channel_id=1, source_target_pairs={{0,31},{1,32},{2,33},{3,34},{4,35},{5,36},{6,37},{7,38},{8,39},{9,... | collective-permute-start | bytes 147464
  1527.7 7.0 collective-permute-start.21
  1571.5 3.9 collective-permute-start.5
  1648.2 3.8 collective-permute-start.37
  1654.0 4.2 collective-permute-start.35
  1700.8 68.8 %psum.15 = f32[]{:T(128)} all-reduce(f32[]{:T(128)S(6)} %add.151), channel_id=1, replica_groups=mesh['grp'=2,'dp'=64] {'grp','dp'}, use_global_device_ids=true, to_apply=%region_17.0 | all-reduce | flops 1 | bytes 8 | tf_op jit(solution)/shard_map/psum | solution.py:176
  1770.3 5.6 concatenate
  1776.0 4.3 collective-permute-start.73
  1786.8 4.0 collective-permute-start.70
  1790.8 6.5 collective-permute-start.69
  1798.0 24.2 %concatenate.1 = f32[524,768]{1,0:T(8,128)S(1)} concatenate(f32[12,768]{1,0:T(8,128)S(1)} %collective-permute-done.63, f32[16,768]{1,0:T(8,128)S(1)} %collective-permute-done.62, f32[16,768]{1,0:T(8,128)S(1)} %collective-permute-done.61, f32[16,768]{1,0:T(8,128)S(1)} %collective-permute-done.60, f32[16,768]{1,0:T(8,128)S(1)} %collective-permute-done.59, f32[16,768]{1,0:T(8,128)} %copy-done.9, ...), dimensions={0} | concatenate | bytes 3219456
  1824.2 4.0 collective-permute-start.67
  1831.0 5.3 collective-permute-start.65
  1842.3 4.0 collective-permute-done.64
  1846.3 6.8 concatenate.2
  (349 shorter events, 232.4 us)
Async XLA Ops:
  7.2 171.7 %all-reduce.13.cloned.1.call-start = ((), (), s32[]{:S(2)}) async-start(), calls=%async_computation.2 | async-start | bytes 524288 | tf_op jit(solution)/shard_map/psum | solution.py:110
  10.8 343.0 %all-gather.16.cloned.1.call-start = ((), (), s32[]{:S(2)}) async-start(), calls=%async_computation.4 | async-start | bytes 3170304 | tf_op jit(solution)/shard_map/all_gather | solution.py:83
  11.5 539.4 %all-gather.14.cloned.1.call-start = ((), (), s32[]{:S(2)}) async-start(), calls=%async_computation.3 | async-start | bytes 3170304 | tf_op jit(solution)/shard_map/all_gather | solution.py:79
  12.3 728.2 %all-gather.22.cloned.1.call-start = ((), (), s32[]{:S(2)}) async-start(), calls=%async_computation.7 | async-start | bytes 8519680 | tf_op jit(solution)/shard_map/all_gather | solution.py:60
  12.8 736.7 %all-gather.20.cloned.1.call-start = ((), (), s32[]{:S(2)}) async-start(), calls=%async_computation.6 | async-start | bytes 8519680 | tf_op jit(solution)/shard_map/all_gather | solution.py:54
  13.4 876.4 %all-reduce.15.cloned.1.call-start = ((), (), s32[]{:S(2)}) async-start(), calls=%async_computation.8 | async-start | bytes 524288
  735.7 350.2 %all-gather.18.cloned.1.call-start = ((), (), s32[]{:S(2)}) async-start(), calls=%async_computation.5 | async-start | bytes 3170304 | tf_op jit(solution)/shard_map/all_gather | solution.py:84
  736.4 381.1 %reduce-scatter.8.cloned.1.call-start = ((), (), s32[]{:S(2)}) async-start(), calls=%async_computation.1 | async-start | bytes 2555904 | tf_op jit(solution)/shard_map/reduce_scatter | solution.py:64
  773.3 926.2 %all-reduce.17.cloned.1.call-start = ((), (), s32[]{:S(2)}) async-start(), calls=%async_computation.9 | async-start | bytes 3145728
  1472.1 45.7 %collective-permute-start.87 = (f32[768,13]{0,1:T(8,128)S(1)}, f32[768,13]{0,1:T(8,128)S(1)}, u32[]{:S(2)}, u32[]{:S(2)}) collective-permute-start(f32[768,13]{0,1:T(8,128)S(1)} %slice.2), channel_id=1, source_target_pairs={{0,24},{1,25},{2,26},{3,27},{4,28},{5,29},{6,30},{7,31},{8,32},{9,... | collective-permute-start | bytes 119816
  1474.1 39.9 %collective-permute-start.31 = (f32[768,12]{0,1:T(8,128)S(1)}, f32[768,12]{0,1:T(8,128)S(1)}, u32[]{:S(2)}, u32[]{:S(2)}) collective-permute-start(f32[768,12]{0,1:T(8,128)S(1)} %slice), channel_id=1, source_target_pairs={{0,32},{1,33},{2,34},{3,35},{4,36},{5,37},{6,38},{7,39},{8,40},{9,... | collective-permute-start | bytes 110600
  1476.0 39.9 %collective-permute-start.63 = (f32[12,768]{1,0:T(8,128)S(1)}, f32[12,768]{1,0:T(8,128)S(1)}, u32[]{:S(2)}, u32[]{:S(2)}) collective-permute-start(f32[12,768]{1,0:T(8,128)S(1)} %slice.1), channel_id=1, source_target_pairs={{0,32},{1,33},{2,34},{3,35},{4,36},{5,37},{6,38},{7,39},{8,40},{9,... | collective-permute-start | bytes 110600
  1485.8 34.0 %collective-permute-start.30 = (f32[768,16]{0,1:T(8,128)S(1)}, f32[768,16]{0,1:T(8,128)S(1)}, u32[]{:S(2)}, u32[]{:S(2)}) collective-permute-start(f32[768,16]{0,1:T(8,128)S(1)} %get-tuple-element.14), channel_id=1, source_target_pairs={{0,31},{1,32},{2,33},{3,34},{4,35},{5,36},{6,37},{7,38},{8,39},{9,... | collective-permute-start | bytes 147464
  1523.7 15.2 collective-permute-start.23
  1525.8 15.0 collective-permute-start.22
  1527.7 15.1 collective-permute-start.21
  1671.5 15.9 collective-permute-start.83
  1673.9 15.9 collective-permute-start.82
  1676.4 16.1 collective-permute-start.81
  1679.2 16.0 collective-permute-start.80
  1682.0 15.5 collective-permute-start.79
  1687.5 88.5 %collective-permute-start.78 = (f32[768,16]{0,1:T(8,128)S(1)}, f32[768,16]{0,1:T(8,128)}, u32[]{:S(2)}, u32[]{:S(2)}) collective-permute-start(f32[768,16]{0,1:T(8,128)S(1)} %get-tuple-element.16), channel_id=1, source_target_pairs={{0,15},{1,16},{2,17},{3,18},{4,19},{5,20},{6,21},{7,22},{8,23},{9,... | collective-permute-start | bytes 147464
  1689.8 90.5 %collective-permute-start.77 = (f32[768,16]{0,1:T(8,128)S(1)}, f32[768,16]{0,1:T(8,128)}, u32[]{:S(2)}, u32[]{:S(2)}) collective-permute-start(f32[768,16]{0,1:T(8,128)S(1)} %get-tuple-element.16), channel_id=1, source_target_pairs={{0,14},{1,15},{2,16},{3,17},{4,18},{5,19},{6,20},{7,21},{8,22},{9,... | collective-permute-start | bytes 147464
  1692.6 91.3 %collective-permute-start.76 = (f32[768,16]{0,1:T(8,128)S(1)}, f32[768,16]{0,1:T(8,128)}, u32[]{:S(2)}, u32[]{:S(2)}) collective-permute-start(f32[768,16]{0,1:T(8,128)S(1)} %get-tuple-element.16), channel_id=1, source_target_pairs={{0,13},{1,14},{2,15},{3,16},{4,17},{5,18},{6,19},{7,20},{8,21},{9,... | collective-permute-start | bytes 147464
  1695.2 91.6 %collective-permute-start.75 = (f32[768,16]{0,1:T(8,128)S(1)}, f32[768,16]{0,1:T(8,128)}, u32[]{:S(2)}, u32[]{:S(2)}) collective-permute-start(f32[768,16]{0,1:T(8,128)S(1)} %get-tuple-element.16), channel_id=1, source_target_pairs={{0,12},{1,13},{2,14},{3,15},{4,16},{5,17},{6,18},{7,19},{8,20},{9,... | collective-permute-start | bytes 147464
  1697.5 93.4 %collective-permute-start.74 = (f32[768,16]{0,1:T(8,128)S(1)}, f32[768,16]{0,1:T(8,128)}, u32[]{:S(2)}, u32[]{:S(2)}) collective-permute-start(f32[768,16]{0,1:T(8,128)S(1)} %get-tuple-element.16), channel_id=1, source_target_pairs={{0,11},{1,12},{2,13},{3,14},{4,15},{5,16},{6,17},{7,18},{8,19},{9,... | collective-permute-start | bytes 147464
  1776.0 46.2 %collective-permute-start.73 = (f32[768,16]{0,1:T(8,128)S(1)}, f32[768,16]{0,1:T(8,128)S(1)}, u32[]{:S(2)}, u32[]{:S(2)}) collective-permute-start(f32[768,16]{0,1:T(8,128)S(1)} %get-tuple-element.16), channel_id=1, source_target_pairs={{0,10},{1,11},{2,12},{3,13},{4,14},{5,15},{6,16},{7,17},{8,18},{9,... | collective-permute-start | bytes 147464
  1780.3 43.9 %collective-permute-start.72 = (f32[768,16]{0,1:T(8,128)S(1)}, f32[768,16]{0,1:T(8,128)S(1)}, u32[]{:S(2)}, u32[]{:S(2)}) collective-permute-start(f32[768,16]{0,1:T(8,128)S(1)} %get-tuple-element.16), channel_id=1, source_target_pairs={{0,9},{1,10},{2,11},{3,12},{4,13},{5,14},{6,15},{7,16},{8,17},{9,1... | collective-permute-start | bytes 147464
  1783.9 44.3 %collective-permute-start.71 = (f32[768,16]{0,1:T(8,128)S(1)}, f32[768,16]{0,1:T(8,128)S(1)}, u32[]{:S(2)}, u32[]{:S(2)}) collective-permute-start(f32[768,16]{0,1:T(8,128)S(1)} %get-tuple-element.16), channel_id=1, source_target_pairs={{0,8},{1,9},{2,10},{3,11},{4,12},{5,13},{6,14},{7,15},{8,16},{9,17... | collective-permute-start | bytes 147464
  1786.8 44.1 %collective-permute-start.70 = (f32[768,16]{0,1:T(8,128)S(1)}, f32[768,16]{0,1:T(8,128)S(1)}, u32[]{:S(2)}, u32[]{:S(2)}) collective-permute-start(f32[768,16]{0,1:T(8,128)S(1)} %get-tuple-element.16), channel_id=1, source_target_pairs={{0,7},{1,8},{2,9},{3,10},{4,11},{5,12},{6,13},{7,14},{8,15},{9,16}... | collective-permute-start | bytes 147464
  1790.8 45.4 %collective-permute-start.69 = (f32[768,16]{0,1:T(8,128)S(1)}, f32[768,16]{0,1:T(8,128)S(1)}, u32[]{:S(2)}, u32[]{:S(2)}) collective-permute-start(f32[768,16]{0,1:T(8,128)S(1)} %get-tuple-element.16), channel_id=1, source_target_pairs={{0,6},{1,7},{2,8},{3,9},{4,10},{5,11},{6,12},{7,13},{8,14},{9,15},... | collective-permute-start | bytes 147464
  1822.2 16.6 collective-permute-start.68
  (120 other events, 3581.7 us)
Sparse Core Ops, SparseCore 0:
  12.7 144.8 all-reduce.12
  159.4 194.4 all-gather.15
  355.6 195.2 all-gather.13
  554.0 80.3 all-gather.21
  637.5 80.1 all-gather.19
  735.8 154.0 all-reduce.14
  891.6 194.2 all-gather.17
  1088.2 29.3 reduce-scatter.7
  1122.3 152.8 all-reduce.16
where the time goes:
time: 1870 us; the launch traced here: 1860 us
  blocking collectives  730 us (39%)
  waiting for transfers between devices  715 us (38%)
  starting transfers between devices  252 us (13%)
  local copies, waits for them, and re-layouts  80.9 us (4%)
  matrix products  41.4 us (2%)
  between operations  24.5 us (1%)
    unnamed x1, blocking collectives  336 us
    unnamed x90, starting transfers between devices  252 us
    all_gather x1, waiting for transfers between devices, local(): lax.all_gather(student_up, ('grp', 'dp'), axis=1, tiled=True)  192 us
    all_gather x1, waiting for transfers between devices, local(): lax.all_gather(student_head, ('grp', 'dp'), axis=1, tiled=True)  192 us
    all_gather x1, waiting for transfers between devices, local(): lax.all_gather(student_down, ('grp', 'dp'), axis=0, tiled=True)  173 us
    all_gather x1, blocking collectives, local(): lax.all_gather(student_proj, ('grp', 'dp'), axis=1, tiled=True)  164 us
    all_gather x1, blocking collectives, local(): gathered = lax.all_gather(image_emb, ('grp', 'dp'), axis=0, tiled=True)  161 us
    unnamed x99, waiting for transfers between devices  132 us
  transfers between devices with their start and end apart: 97, of which 15 were waited for; matrix products, arithmetic and copies ran while one was open for 25% of the time, Pallas kernels for 0%

commit v1 on v0

--- a/solution.py
+++ b/solution.py
@@ -81,7 +81,12 @@
     )
     down_whole, head_whole, proj_whole = (
         lax.all_gather(student_down, ("grp", "dp"), axis=0, tiled=True),
-        lax.all_gather(student_head, ("grp", "dp"), axis=1, tiled=True),
+        jnp.concatenate(
+            lax.all_to_all(
+                jnp.stack([student_head] * lax.axis_size(("grp", "dp"))), ("grp", "dp"), 0, 0
+            ),
+            axis=1,
+        ),
         lax.all_gather(student_proj, ("grp", "dp"), axis=1, tiled=True),
     )
     student_act = gelu_tanh(gate_out).astype(jnp.bfloat16)

time: 1870 us -> 1710 us (0.914)
  waiting for transfers between devices: 715 us -> 494 us
  blocking collectives: 730 us -> 768 us
    all_gather x1 -> x0, waiting for transfers between devices: 192 us -> none  [local(): lax.all_gather(student_head, ('grp', 'dp'), axis=1, tiled=True)]
    all_gather x1, blocking collectives: 164 us -> 202 us  [local(): lax.all_gather(student_proj, ('grp', 'dp'), axis=1, tiled=True)]
    all_gather x1, waiting for transfers between devices: 173 us -> 144 us  [local(): lax.all_gather(student_down, ('grp', 'dp'), axis=0, tiled=True)]
    unnamed x127 -> x140, local copies, waits for them, and re-layouts: 75.7 us -> 73 us
    unnamed x99 -> x98, waiting for transfers between devices: 132 us -> 132 us
  transfers between devices with their start and end apart: 97 -> 97, of which waited for: 15 -> 14; matrix products, arithmetic and copies ran while one was open for 25% -> 28% of each run, Pallas kernels for 0% -> 0%
where the time goes in v1:
time: 1710 us; the launch traced here: 1700 us
  blocking collectives  768 us (45%)
  waiting for transfers between devices  494 us (29%)
  starting transfers between devices  262 us (15%)
  local copies, waits for them, and re-layouts  85 us (5%)
  matrix products  44 us (3%)
  between operations  25.1 us (1%)
  other arithmetic  18.9 us (1%)
    unnamed x1, blocking collectives  336 us
    unnamed x90, starting transfers between devices  251 us
    all_gather x1, blocking collectives, local(): lax.all_gather(student_proj, ('grp', 'dp'), axis=1, tiled=True)  202 us
    all_gather x1, waiting for transfers between devices, local(): lax.all_gather(student_up, ('grp', 'dp'), axis=1, tiled=True)  192 us
    all_gather x1, blocking collectives, local(): gathered = lax.all_gather(image_emb, ('grp', 'dp'), axis=0, tiled=True)  162 us
    all_gather x1, waiting for transfers between devices, local(): lax.all_gather(student_down, ('grp', 'dp'), axis=0, tiled=True)  144 us
    unnamed x98, waiting for transfers between devices  132 us
    unnamed x140, local copies, waits for them, and re-layouts  73 us
  transfers between devices with their start and end apart: 97, of which 14 were waited for; matrix products, arithmetic and copies ran while one was open for 28% of the time, Pallas kernels for 0%

profile of v1, /device:TPU:16, one launch (start us, length us, event | category | flops | bytes accessed | tf_op | source)
XLA Modules:
  0.0 1697.1 jit_solution(18348688529134525293)
XLA Ops:
  16.1 10.3 all-to-all-start
  26.5 201.6 %all-gather.5 = bf16[128,4,768]{2,1,0:T(4,128)(2,1)} all-gather(bf16[1,4,768]{2,1,0:T(4,128)(2,1)S(1)} %bitcast.97), channel_id=1, replica_groups=mesh['grp'=2,'dp'=64] {'grp','dp'}, dimensions={0}, use_global_device_ids=true | all-gather | bytes 792576 | tf_op jit(solution)/shard_map/all_gather | solution.py:90
  238.0 144.5 %all-gather.14.cloned.1.call-done = bf16[128,12,768]{2,1,0:T(8,128)(2,1)} async-done(((bf16[1,12,768]{2,1,0:T(8,128)(2,1)}), bf16[128,12,768]{2,1,0:T(8,128)(2,1)}) %all-gather.14.cloned.1.call-update) | async-done | bytes 2359312 | tf_op jit(solution)/shard_map/all_gather | solution.py:83
  382.5 4.9 reshape.204
  387.4 192.1 %all-gather.12.cloned.1.call-done = bf16[128,12,768]{2,1,0:T(8,128)(2,1)} async-done(((bf16[1,12,768]{2,1,0:T(8,128)(2,1)}), bf16[128,12,768]{2,1,0:T(8,128)(2,1)}) %all-gather.12.cloned.1.call-update) | async-done | bytes 2359312 | tf_op jit(solution)/shard_map/all_gather | solution.py:79
  579.5 4.9 reshape.202
  592.4 161.6 %all-gather.6 = f32[128,1,512]{2,1,0:T(1,128)S(1)} all-gather(f32[1,1,512]{2,1,0:T(1,128)S(1)} %bitcast.85), channel_id=2, replica_groups=mesh['grp'=2,'dp'=64] {'grp','dp'}, dimensions={0}, use_global_device_ids=true | all-gather | bytes 264192 | tf_op jit(solution)/shard_map/all_gather | solution.py:118
  769.3 9.1 reshape.208
  778.5 9.1 reshape.206
  787.6 14.7 convolution_convert_fusion
  807.0 114.9 %all-reduce.15.cloned.1.call-done = f32[128,512]{1,0:T(8,128)} async-done(((f32[128,512]{1,0:T(8,128)}), f32[128,512]{1,0:T(8,128)}) %all-reduce.15.cloned.1.call-update) | async-done | bytes 262160
  927.4 25.2 %reduce-scatter.8.cloned.1.call-done = bf16[256,1664]{1,0:T(8,128)(2,1)} async-done(((bf16[512,1664]{1,0:T(8,128)(2,1)}), bf16[256,1664]{1,0:T(8,128)(2,1)}) %reduce-scatter.8.cloned.1.call-update) | async-done | bytes 851984 | tf_op jit(solution)/shard_map/reduce_scatter | solution.py:64
  959.0 6.2 fusion.45
  971.7 335.7 %fusion.88 = (f32[768,16]{0,1:T(8,128)S(1)}, f32[16,768]{1,0:T(8,128)S(1)}, f32[768,16]{0,1:T(8,128)S(1)}) fusion(f32[768,1536]{0,1:T(8,128)} %fusion.45, f32[1536,768]{1,0:T(8,128)} %fusion.87, f32[768,1664]{0,1:T(8,128)} %fusion.56), kind=kCustom, calls=%all-reduce-scatter.3 | all-reduce-scatter fusion | flops 4718593 | bytes 14696448
  1311.3 9.6 collective-permute-start.63
  1320.9 26.3 %collective-permute-start.30 = (f32[768,16]{0,1:T(8,128)S(1)}, f32[768,16]{0,1:T(8,128)S(1)}, u32[]{:S(2)}, u32[]{:S(2)}) collective-permute-start(f32[768,16]{0,1:T(8,128)S(1)} %get-tuple-element.14), channel_id=1, source_target_pairs={{0,31},{1,32},{2,33},{3,34},{4,35},{5,36},{6,37},{7,38},{8,39},{9,... | collective-permute-start | bytes 147464
  1362.9 7.0 collective-permute-start.21
  1406.7 3.9 collective-permute-start.5
  1412.8 3.7 collective-permute-start.3
  1475.3 3.8 collective-permute-start.40
  1483.4 3.8 collective-permute-start.37
  1489.2 4.2 collective-permute-start.35
  1536.0 68.8 %psum.15 = f32[]{:T(128)} all-reduce(f32[]{:T(128)S(6)} %add.151), channel_id=1, replica_groups=mesh['grp'=2,'dp'=64] {'grp','dp'}, use_global_device_ids=true, to_apply=%region_17.0 | all-reduce | flops 1 | bytes 8 | tf_op jit(solution)/shard_map/psum | solution.py:181
  1605.5 5.6 concatenate
  1611.1 4.3 collective-permute-start.73
  1622.0 4.0 collective-permute-start.70
  1626.0 6.5 collective-permute-start.69
  1633.2 24.2 %concatenate.1 = f32[524,768]{1,0:T(8,128)S(1)} concatenate(f32[12,768]{1,0:T(8,128)S(1)} %collective-permute-done.63, f32[16,768]{1,0:T(8,128)S(1)} %collective-permute-done.62, f32[16,768]{1,0:T(8,128)S(1)} %collective-permute-done.61, f32[16,768]{1,0:T(8,128)S(1)} %collective-permute-done.60, f32[16,768]{1,0:T(8,128)S(1)} %collective-permute-done.59, f32[16,768]{1,0:T(8,128)} %copy-done.14, ...), dimensions={0} | concatenate | bytes 3219456
  1659.3 4.0 collective-permute-start.67
  1666.1 5.3 collective-permute-start.65
  1677.4 4.0 collective-permute-done.64
  1681.4 6.8 concatenate.2
  (363 shorter events, 241.5 us)
Async XLA Ops:
  7.2 228.7 %all-reduce.13.cloned.1.call-start = ((), (), s32[]{:S(2)}) async-start(), calls=%async_computation.3 | async-start | bytes 524288 | tf_op jit(solution)/shard_map/psum | solution.py:115
  10.8 371.8 %all-gather.14.cloned.1.call-start = ((), (), s32[]{:S(2)}) async-start(), calls=%async_computation.5 | async-start | bytes 3170304 | tf_op jit(solution)/shard_map/all_gather | solution.py:83
  11.5 568.0 %all-gather.12.cloned.1.call-start = ((), (), s32[]{:S(2)}) async-start(), calls=%async_computation.4 | async-start | bytes 3170304 | tf_op jit(solution)/shard_map/all_gather | solution.py:79
  12.3 757.1 %all-gather.18.cloned.1.call-start = ((), (), s32[]{:S(2)}) async-start(), calls=%async_computation.7 | async-start | bytes 8519680 | tf_op jit(solution)/shard_map/all_gather | solution.py:60
  12.8 765.6 %all-gather.16.cloned.1.call-start = ((), (), s32[]{:S(2)}) async-start(), calls=%async_computation.6 | async-start | bytes 8519680 | tf_op jit(solution)/shard_map/all_gather | solution.py:54
  16.1 786.4 %all-to-all-start = ((bf16[128,768,13]{1,2,0:T(8,128)(2,1)}), bf16[128,768,13]{1,2,0:T(8,128)(2,1)S(1)}, u32[]{:S(2)}, u32[]{:S(2)}) async-start(bf16[128,768,13]{1,2,0:T(8,128)(2,1)} %stack.2), calls=%async_computation | async-start | bytes 6291456 | tf_op jit(solution)/shard_map/all_to_all | solution.py:85
  26.4 895.4 %all-reduce.15.cloned.1.call-start = ((), (), s32[]{:S(2)}) async-start(), calls=%async_computation.8 | async-start | bytes 524288
  768.8 183.8 %reduce-scatter.8.cloned.1.call-start = ((), (), s32[]{:S(2)}) async-start(), calls=%async_computation.2 | async-start | bytes 2555904 | tf_op jit(solution)/shard_map/reduce_scatter | solution.py:64
  802.3 732.4 %all-reduce.17.cloned.1.call-start = ((), (), s32[]{:S(2)}) async-start(), calls=%async_computation.9 | async-start | bytes 3145728
  1307.4 45.6 %collective-permute-start.87 = (f32[768,13]{0,1:T(8,128)S(1)}, f32[768,13]{0,1:T(8,128)S(1)}, u32[]{:S(2)}, u32[]{:S(2)}) collective-permute-start(f32[768,13]{0,1:T(8,128)S(1)} %slice.2), channel_id=1, source_target_pairs={{0,24},{1,25},{2,26},{3,27},{4,28},{5,29},{6,30},{7,31},{8,32},{9,... | collective-permute-start | bytes 119816
  1309.4 39.8 %collective-permute-start.31 = (f32[768,12]{0,1:T(8,128)S(1)}, f32[768,12]{0,1:T(8,128)S(1)}, u32[]{:S(2)}, u32[]{:S(2)}) collective-permute-start(f32[768,12]{0,1:T(8,128)S(1)} %slice), channel_id=1, source_target_pairs={{0,32},{1,33},{2,34},{3,35},{4,36},{5,37},{6,38},{7,39},{8,40},{9,... | collective-permute-start | bytes 110600
  1311.3 39.8 %collective-permute-start.63 = (f32[12,768]{1,0:T(8,128)S(1)}, f32[12,768]{1,0:T(8,128)S(1)}, u32[]{:S(2)}, u32[]{:S(2)}) collective-permute-start(f32[12,768]{1,0:T(8,128)S(1)} %slice.1), channel_id=1, source_target_pairs={{0,32},{1,33},{2,34},{3,35},{4,36},{5,37},{6,38},{7,39},{8,40},{9,... | collective-permute-start | bytes 110600
  1320.9 34.0 %collective-permute-start.30 = (f32[768,16]{0,1:T(8,128)S(1)}, f32[768,16]{0,1:T(8,128)S(1)}, u32[]{:S(2)}, u32[]{:S(2)}) collective-permute-start(f32[768,16]{0,1:T(8,128)S(1)} %get-tuple-element.14), channel_id=1, source_target_pairs={{0,31},{1,32},{2,33},{3,34},{4,35},{5,36},{6,37},{7,38},{8,39},{9,... | collective-permute-start | bytes 147464
  1358.9 15.2 collective-permute-start.23
  1361.0 15.0 collective-permute-start.22
  1362.9 15.1 collective-permute-start.21
  1506.7 15.9 collective-permute-start.83
  1509.0 16.1 collective-permute-start.82
  1511.6 16.1 collective-permute-start.81
  1514.3 16.0 collective-permute-start.80
  1517.2 15.4 collective-permute-start.79
  1522.7 88.5 %collective-permute-start.78 = (f32[768,16]{0,1:T(8,128)S(1)}, f32[768,16]{0,1:T(8,128)}, u32[]{:S(2)}, u32[]{:S(2)}) collective-permute-start(f32[768,16]{0,1:T(8,128)S(1)} %get-tuple-element.16), channel_id=1, source_target_pairs={{0,15},{1,16},{2,17},{3,18},{4,19},{5,20},{6,21},{7,22},{8,23},{9,... | collective-permute-start | bytes 147464
  1525.2 90.3 %collective-permute-start.77 = (f32[768,16]{0,1:T(8,128)S(1)}, f32[768,16]{0,1:T(8,128)}, u32[]{:S(2)}, u32[]{:S(2)}) collective-permute-start(f32[768,16]{0,1:T(8,128)S(1)} %get-tuple-element.16), channel_id=1, source_target_pairs={{0,14},{1,15},{2,16},{3,17},{4,18},{5,19},{6,20},{7,21},{8,22},{9,... | collective-permute-start | bytes 147464
  1527.8 91.3 %collective-permute-start.76 = (f32[768,16]{0,1:T(8,128)S(1)}, f32[768,16]{0,1:T(8,128)}, u32[]{:S(2)}, u32[]{:S(2)}) collective-permute-start(f32[768,16]{0,1:T(8,128)S(1)} %get-tuple-element.16), channel_id=1, source_target_pairs={{0,13},{1,14},{2,15},{3,16},{4,17},{5,18},{6,19},{7,20},{8,21},{9,... | collective-permute-start | bytes 147464
  1530.3 91.7 %collective-permute-start.75 = (f32[768,16]{0,1:T(8,128)S(1)}, f32[768,16]{0,1:T(8,128)}, u32[]{:S(2)}, u32[]{:S(2)}) collective-permute-start(f32[768,16]{0,1:T(8,128)S(1)} %get-tuple-element.16), channel_id=1, source_target_pairs={{0,12},{1,13},{2,14},{3,15},{4,16},{5,17},{6,18},{7,19},{8,20},{9,... | collective-permute-start | bytes 147464
  1532.6 93.4 %collective-permute-start.74 = (f32[768,16]{0,1:T(8,128)S(1)}, f32[768,16]{0,1:T(8,128)}, u32[]{:S(2)}, u32[]{:S(2)}) collective-permute-start(f32[768,16]{0,1:T(8,128)S(1)} %get-tuple-element.16), channel_id=1, source_target_pairs={{0,11},{1,12},{2,13},{3,14},{4,15},{5,16},{6,17},{7,18},{8,19},{9,... | collective-permute-start | bytes 147464
  1611.1 46.2 %collective-permute-start.73 = (f32[768,16]{0,1:T(8,128)S(1)}, f32[768,16]{0,1:T(8,128)S(1)}, u32[]{:S(2)}, u32[]{:S(2)}) collective-permute-start(f32[768,16]{0,1:T(8,128)S(1)} %get-tuple-element.16), channel_id=1, source_target_pairs={{0,10},{1,11},{2,12},{3,13},{4,14},{5,15},{6,16},{7,17},{8,18},{9,... | collective-permute-start | bytes 147464
  1615.5 43.9 %collective-permute-start.72 = (f32[768,16]{0,1:T(8,128)S(1)}, f32[768,16]{0,1:T(8,128)S(1)}, u32[]{:S(2)}, u32[]{:S(2)}) collective-permute-start(f32[768,16]{0,1:T(8,128)S(1)} %get-tuple-element.16), channel_id=1, source_target_pairs={{0,9},{1,10},{2,11},{3,12},{4,13},{5,14},{6,15},{7,16},{8,17},{9,1... | collective-permute-start | bytes 147464
  1619.0 44.3 %collective-permute-start.71 = (f32[768,16]{0,1:T(8,128)S(1)}, f32[768,16]{0,1:T(8,128)S(1)}, u32[]{:S(2)}, u32[]{:S(2)}) collective-permute-start(f32[768,16]{0,1:T(8,128)S(1)} %get-tuple-element.16), channel_id=1, source_target_pairs={{0,8},{1,9},{2,10},{3,11},{4,12},{5,13},{6,14},{7,15},{8,16},{9,17... | collective-permute-start | bytes 147464
  1622.0 44.1 %collective-permute-start.70 = (f32[768,16]{0,1:T(8,128)S(1)}, f32[768,16]{0,1:T(8,128)S(1)}, u32[]{:S(2)}, u32[]{:S(2)}) collective-permute-start(f32[768,16]{0,1:T(8,128)S(1)} %get-tuple-element.16), channel_id=1, source_target_pairs={{0,7},{1,8},{2,9},{3,10},{4,11},{5,12},{6,13},{7,14},{8,15},{9,16}... | collective-permute-start | bytes 147464
  1626.0 45.4 %collective-permute-start.69 = (f32[768,16]{0,1:T(8,128)S(1)}, f32[768,16]{0,1:T(8,128)S(1)}, u32[]{:S(2)}, u32[]{:S(2)}) collective-permute-start(f32[768,16]{0,1:T(8,128)S(1)} %get-tuple-element.16), channel_id=1, source_target_pairs={{0,6},{1,7},{2,8},{3,9},{4,10},{5,11},{6,12},{7,13},{8,14},{9,15},... | collective-permute-start | bytes 147464
  1657.4 16.6 collective-permute-start.68
  (127 other events, 3703.3 us)
Sparse Core Ops, SparseCore 0:
  12.7 173.7 all-reduce.12
  188.2 194.2 all-gather.13
  384.2 195.2 all-gather.11
  582.6 80.4 all-gather.17
  666.2 80.2 all-gather.15
  768.9 152.8 all-reduce.14
  924.2 28.3 reduce-scatter.7
  957.3 153.6 all-reduce.16
